TPU v7x, 32 devices: a whole 2x2x4 slice. The times are simulated.
32 devices in a mesh: gx: 8 (over y, x, core), gy: 4 (over z).
Axes of the slice: x: 2, y: 2, z: 4, core: 2. Of those that a mesh axis runs over, the one named last changes fastest.
Arguments:
- products: bfloat16 [1536, 3, 2048], P('gy', None, 'gx'), may hold values from -6 to 6
- operator: bfloat16 [1536, 1536], P(None, 'gy'), may hold values from -0.21875 to 0.21875
Outputs:
- derivative: bfloat16 [1536, 3, 2048], P(('gy', 'gx'))
All inputs are finite; a program needn't handle non-finite values.
Results may differ from a plain program's by a relative error of at most 0.002.
Values may be sent and summed in bfloat16 or wider, within the bound.
No kernel may reach another device: no remote copies, remote signals or barrier semaphores. Data moves between devices by JAX's collectives and lax.ppermute only.
A program may use at most 64 MiB of HBM per device.

v0:
```python
import jax
import jax.numpy as jnp
from jax import lax
from jax.sharding import PartitionSpec as P


def body(products, operator):
    y_local, three, m_local = products.shape
    flat = products.reshape(y_local, three * m_local)
    summed = lax.psum_scatter(
        jnp.dot(operator, flat, preferred_element_type=jnp.float32),
        "gy",
        scatter_dimension=0,
        tiled=True,
    )
    result = summed.astype(jnp.bfloat16).reshape(y_local, three, m_local)
    return lax.all_to_all(result, "gx", split_axis=0, concat_axis=2, tiled=True)


def solution(mesh):
    return jax.shard_map(
        body,
        mesh=mesh,
        in_specs=(P("gy", None, "gx"), P(None, "gy")),
        out_specs=P(("gy", "gx"), None, None),
        check_vma=False,
    )
```

profile of v0, /device:TPU:0, one launch (start us, length us, event | category | flops | bytes accessed | tf_op | source)
XLA Modules:
  0.0 125.9 jit_solution(14700882482431408080)
XLA Ops:
  6.5 0.0 copy-start
  6.5 0.0 reduce-scatter.2.cloned.1.call-start
  6.5 1.5 %copy.14 = bf16[384,3,256]{0,2,1:T(8,128)(2,1)S(1)} copy(bf16[384,3,256]{2,0,1:T(8,128)(2,1)} %param.2) | data formatting | bytes 1179648 | tf_op args[0]
  8.0 0.0 copy-done
  8.0 3.5 %fusion = f32[1536,768]{1,0:T(8,128)} fusion(bf16[1536,384]{1,0:T(8,128)(2,1)S(1)} %copy-done, bf16[384,768]{0,1:T(8,128)(2,1)S(1)} %bitcast.9), kind=kOutput, calls=%fused_computation | convolution fusion | flops 905969664 | bytes 6488064 | tf_op jit(solution)/shard_map/dot_general | solution.py:11
  11.5 0.0 reduce-scatter.2.cloned.1.call-update
  11.6 88.2 %reduce-scatter.2.cloned.1.call-done = f32[384,768]{1,0:T(8,128)} async-done(((f32[1536,768]{1,0:T(8,128)}), f32[384,768]{1,0:T(8,128)}) %reduce-scatter.2.cloned.1.call-update) | async-done | bytes 1179664 | tf_op jit(solution)/shard_map/reduce_scatter | solution.py:10
  99.7 1.3 %convert_element_type.3 = bf16[384,768]{1,0:T(8,128)(2,1)S(1)} convert(f32[384,768]{1,0:T(8,128)} %reduce-scatter.2.cloned.1.call-done) | non-fusion elementwise | flops 294912 | bytes 1769472 | tf_op jit(solution)/shard_map/convert_element_type | solution.py:16
  101.1 0.3 copy.15
  101.4 0.8 copy.16
  102.2 16.0 %all_to_all.18 = bf16[384,3,256]{2,1,0:T(4,128)(2,1)S(1)} all-to-all(bf16[384,3,256]{2,1,0:T(4,128)(2,1)S(1)} %copy.16), channel_id=1, replica_groups=mesh['gx'=8,'gy'=4] {'gx'}, dimensions={0} | all-to-all | bytes 1179648 | tf_op jit(solution)/shard_map/all_to_all | solution.py:17
  118.1 0.1 copy.17
  118.2 0.9 copy.19
Async XLA Ops:
  6.5 1.5 %copy-start = (bf16[1536,384]{1,0:T(8,128)(2,1)S(1)}, bf16[1536,384]{1,0:T(8,128)(2,1)}, u32[]{:S(2)}) copy-start(bf16[1536,384]{1,0:T(8,128)(2,1)} %param.3) | copy-start | bytes 3538948
  6.5 93.2 %reduce-scatter.2.cloned.1.call-start = ((), (), s32[]{:S(2)}) async-start(), calls=%async_computation.2 | async-start | bytes 5898240 | tf_op jit(solution)/shard_map/reduce_scatter | solution.py:10
Sparse Core Ops, SparseCore 0:
  11.7 88.0 reduce-scatter.1
where the time goes:
time: 126 us
  waiting for transfers between devices  88.2 us (70%)
  blocking collectives  16 us (13%)
  between operations  13.4 us (11%)
  matrix products  3.53 us (3%)
  local copies, waits for them, and re-layouts  3.49 us (3%)
  other arithmetic  1.33 us (1%)
    reduce_scatter x1, waiting for transfers between devices, body(): lax.psum_scatter(jnp.dot(operator, flat, preferred_element_type=jnp.float...  88.2 us
    all_to_all x1, blocking collectives, body(): return lax.all_to_all(result, 'gx', split_axis=0, concat_axis=2, tiled=True)  16 us
    dot_general x1, matrix products, body(): jnp.dot(operator, flat, preferred_element_type=jnp.float32)  3.53 us
  transfers between devices with their start and end apart: 1, of which 1 were waited for; matrix products, arithmetic and copies ran while one was open for 0% of the time, Pallas kernels for 0%

commit v1 on v0

--- a/solution.py
+++ b/solution.py
@@ -2,6 +2,13 @@
 import jax.numpy as jnp
 from jax import lax
 from jax.sharding import PartitionSpec as P
+
+
+def swap_blocks(x, name, split, join):
+    size = lax.axis_size(name)
+    blocks = jnp.stack(jnp.split(x, size, axis=split), axis=0)
+    blocks = lax.all_to_all(blocks, name, split_axis=0, concat_axis=0)
+    return jnp.concatenate(blocks, axis=join)
 
 
 def body(products, operator):
@@ -14,7 +21,7 @@
         tiled=True,
     )
     result = summed.astype(jnp.bfloat16).reshape(y_local, three, m_local)
-    return lax.all_to_all(result, "gx", split_axis=0, concat_axis=2, tiled=True)
+    return swap_blocks(result, "gx", 0, 2)
 
 
 def solution(mesh):

time: 126 us -> 124 us (0.984)
  blocking collectives: 16 us -> 13.8 us
    all_to_all x1, blocking collectives: 16 us -> 13.8 us  [swap_blocks(): blocks = lax.all_to_all(blocks, name, split_axis=0, concat_axis=0)]
where the time goes in v1:
time: 124 us
  waiting for transfers between devices  88.2 us (71%)
  blocking collectives  13.8 us (11%)
  between operations  13.5 us (11%)
  matrix products  3.53 us (3%)
  local copies, waits for them, and re-layouts  3.14 us (3%)
  other arithmetic  1.33 us (1%)
    reduce_scatter x1, waiting for transfers between devices, body(): lax.psum_scatter(jnp.dot(operator, flat, preferred_element_type=jnp.float...  88.2 us
    all_to_all x1, blocking collectives, swap_blocks(): blocks = lax.all_to_all(blocks, name, split_axis=0, concat_axis=0)  13.8 us
    dot_general x1, matrix products, body(): jnp.dot(operator, flat, preferred_element_type=jnp.float32)  3.53 us
  transfers between devices with their start and end apart: 1, of which 1 were waited for; matrix products, arithmetic and copies ran while one was open for 0% of the time, Pallas kernels for 0%

profile of v1, /device:TPU:0, one launch (start us, length us, event | category | flops | bytes accessed | tf_op | source)
XLA Modules:
  0.0 123.5 jit_solution(17565427176177870618)
XLA Ops:
  6.5 0.0 copy-start
  6.5 0.0 reduce-scatter.2.cloned.1.call-start
  6.5 1.5 %copy.7 = bf16[384,3,256]{0,2,1:T(8,128)(2,1)S(1)} copy(bf16[384,3,256]{2,0,1:T(8,128)(2,1)} %param.2) | data formatting | bytes 1179648 | tf_op args[0]
  8.0 0.0 copy-done
  8.0 3.5 %fusion.1 = f32[1536,768]{1,0:T(8,128)} fusion(bf16[1536,384]{1,0:T(8,128)(2,1)S(1)} %copy-done, bf16[384,768]{0,1:T(8,128)(2,1)S(1)} %bitcast.6), kind=kOutput, calls=%fused_computation.9 | convolution fusion | flops 905969664 | bytes 6488064 | tf_op jit(solution)/shard_map/dot_general | solution.py:18
  11.5 0.0 reduce-scatter.2.cloned.1.call-update
  11.6 88.2 %reduce-scatter.2.cloned.1.call-done = f32[384,768]{1,0:T(8,128)} async-done(((f32[1536,768]{1,0:T(8,128)}), f32[384,768]{1,0:T(8,128)}) %reduce-scatter.2.cloned.1.call-update) | async-done | bytes 1179664 | tf_op jit(solution)/shard_map/reduce_scatter | solution.py:17
  99.7 1.3 %convert_element_type.3 = bf16[384,768]{1,0:T(8,128)(2,1)S(1)} convert(f32[384,768]{1,0:T(8,128)} %reduce-scatter.2.cloned.1.call-done) | non-fusion elementwise | flops 294912 | bytes 1769472 | tf_op jit(solution)/shard_map/convert_element_type | solution.py:23
  101.9 0.1 copy.8
  102.0 13.8 %all_to_all.5 = bf16[8,48,3,256]{3,1,2,0:T(8,128)(2,1)S(1)} all-to-all(bf16[8,48,3,256]{3,1,2,0:T(8,128)(2,1)S(1)} %copy.8), channel_id=1, replica_groups=mesh['gx'=8,'gy'=4] {'gx'}, dimensions={0} | all-to-all | bytes 1179648 | tf_op jit(solution)/shard_map/all_to_all | solution.py:10
  115.8 0.9 copy.10
  (17 shorter events, 0.7 us)
Async XLA Ops:
  6.5 1.5 %copy-start = (bf16[1536,384]{1,0:T(8,128)(2,1)S(1)}, bf16[1536,384]{1,0:T(8,128)(2,1)}, u32[]{:S(2)}) copy-start(bf16[1536,384]{1,0:T(8,128)(2,1)} %param.3) | copy-start | bytes 3538948
  6.5 93.2 %reduce-scatter.2.cloned.1.call-start = ((), (), s32[]{:S(2)}) async-start(), calls=%async_computation.2 | async-start | bytes 5898240 | tf_op jit(solution)/shard_map/reduce_scatter | solution.py:17
Sparse Core Ops, SparseCore 0:
  11.7 88.0 reduce-scatter.1
